TPU v7x, 32 devices: a whole 2x2x4 slice. The times are simulated.
32 devices in a mesh: expert: 4 (over y, core), shard: 8 (over z, x).
Axes of the slice: x: 2, y: 2, z: 4, core: 2. Of those that a mesh axis runs over, the one named last changes fastest.
Arguments:
- train_down: float32 [16, 6400, 4096], P('expert', None, 'shard'), may hold values from -0.109375 to 0.109375
- other_down: bfloat16 [16, 6400, 4096], P('expert', None, 'shard'), may hold values from -0.0390625 to 0.0390625
- router_weight: float32 [4096, 16], P('shard', 'expert'), may hold values from -0.09375 to 0.09375
- router_gain: float32 [4096], P('shard'), may hold values from 0.25 to 1.75
Outputs:
- ready_down: bfloat16 [16, 6400, 4096], P('expert', 'shard')
- scale_down: float32 [16, 6400], P('expert', 'shard')
- serve_router: bfloat16 [4096, 16], replicated
All inputs are finite; a program needn't handle non-finite values.
Results may differ from a plain program's by a relative error of at most 0.001.
Values may be sent and summed in bfloat16 or wider, within the bound.
A program may use at most 256 MiB of HBM per device.

v0:
```python
import jax
import jax.numpy as jnp
from jax import lax
from jax.sharding import PartitionSpec as P


def per_device(train_down, other_down, router_weight, router_gain):
    latest_down = train_down + other_down.astype(jnp.float32)
    total_down = lax.psum(jnp.sum(latest_down * latest_down, axis=2), "shard")
    scale_down = jnp.sqrt(total_down)
    narrow_down = (latest_down / jnp.expand_dims(scale_down, 2)).astype(jnp.bfloat16)
    ready_down = lax.all_to_all(narrow_down, "shard", split_axis=1, concat_axis=2, tiled=True)
    scale_down = lax.dynamic_slice_in_dim(
        scale_down, lax.axis_index("shard") * ready_down.shape[1], ready_down.shape[1], axis=1
    )
    part_router = (router_weight * router_gain[:, None]).astype(jnp.bfloat16)
    row_router = lax.all_gather(part_router, "shard", axis=0, tiled=True)
    serve_router = lax.all_gather(row_router, "expert", axis=1, tiled=True)
    return (ready_down, scale_down, serve_router)


def solution(mesh):
    in_specs = (
        P("expert", None, "shard"),
        P("expert", None, "shard"),
        P("shard", "expert"),
        P("shard"),
    )
    out_specs = (P("expert", "shard", None), P("expert", "shard"), P())
    return jax.shard_map(
        per_device, mesh=mesh, in_specs=in_specs, out_specs=out_specs, check_vma=False
    )
```

profile of v0, /device:TPU:0, one launch (start us, length us, event | category | flops | bytes accessed | tf_op | source)
XLA Modules:
  0.0 905.5 jit_solution(8188198296431997854)
XLA Ops:
  7.2 0.0 all-reduce.2.cloned.1.call-start
  7.2 24.2 %multiply_reduce_fusion = f32[4,6400]{1,0:T(4,128)S(1)} fusion(f32[4,6400,512]{2,1,0:T(8,128)} %param.4, bf16[4,6400,512]{2,1,0:T(8,128)(2,1)} %param.5), kind=kLoop, calls=%fused_computation.1 | loop fusion | flops 52403200 | bytes 78745600 | tf_op jit(solution)/shard_map/reduce_sum | solution.py:9
  31.4 2.3 copy.21
  33.7 0.0 all-reduce.2.cloned.1.call-update
  33.7 135.6 %all-reduce.2.cloned.1.call-done = f32[4,6400]{0,1:T(8,128)} async-done(((f32[4,6400]{0,1:T(8,128)}), f32[4,6400]{0,1:T(8,128)}) %all-reduce.2.cloned.1.call-update) | async-done | bytes 102416 | tf_op jit(solution)/shard_map/psum | solution.py:9
  169.3 2.7 sqrt.3
  172.0 1.2 copy.17
  173.3 34.3 %divide_convert_fusion = bf16[4,6400,512]{2,1,0:T(8,128)(2,1)} fusion(f32[4,6400,512]{2,1,0:T(8,128)} %param.4, bf16[4,6400,512]{2,1,0:T(8,128)(2,1)} %param.5, f32[4,6400]{1,0:T(4,128)S(1)} %copy.17), kind=kLoop, calls=%fused_computation | loop fusion | flops 52428800 | bytes 104960000 | tf_op jit(solution)/shard_map/convert_element_type | solution.py:11
  207.5 33.4 %copy.18 = bf16[4,6400,512]{2,0,1:T(4,128)(2,1)} copy(bf16[4,6400,512]{2,1,0:T(8,128)(2,1)} %divide_convert_fusion) | data formatting | bytes 52428800 | tf_op jit(solution)/shard_map/convert_element_type | solution.py:11
  240.9 0.0 copy-start
  240.9 0.0 copy-start.1
  240.9 6.6 all-to-all-start
  247.6 0.0 copy-done
  247.6 0.0 copy-done.1
  247.6 585.0 %all_gather.6 = bf16[4096,4]{0,1:T(4,128)(2,1)S(1)} all-gather(bf16[512,4]{0,1:T(4,128)(2,1)S(1)} %multiply_convert_fusion), channel_id=1, replica_groups=mesh['expert'=4,'shard'=8] {'shard'}, dimensions={0}, use_global_device_ids=true | all-gather | bytes 36864 | tf_op jit(solution)/shard_map/all_gather | solution.py:17
  832.7 5.4 all-gather
  838.1 0.7 reshape.9
  838.8 0.8 constant_dynamic-slice_fusion
  839.5 1.8 copy.20
  841.3 0.0 all-to-all-done
  841.3 18.2 %copy.19 = bf16[4,800,8,512]{3,2,1,0:T(8,128)(2,1)} copy(bf16[4,800,8,512]{3,0,1,2:T(4,128)(2,1)} %bitcast.1) | data formatting | bytes 52428800 | tf_op jit(solution)/shard_map/all_to_all | solution.py:12
  859.5 39.2 %all_to_all.16 = bf16[4,800,4096]{2,1,0:T(8,128)(2,1)} reshape(bf16[4,800,8,512]{3,2,1,0:T(8,128)(2,1)} %copy.19) | data formatting | bytes 52428800 | tf_op jit(solution)/shard_map/all_to_all | solution.py:12
  (1 shorter events, 0.0 us)
Async XLA Ops:
  7.2 162.2 %all-reduce.2.cloned.1.call-start = ((), (), s32[]{:S(2)}) async-start(), calls=%async_computation.1 | async-start | bytes 6553600 | tf_op jit(solution)/shard_map/psum | solution.py:9
  240.9 6.7 copy-start
  240.9 6.7 copy-start.1
  240.9 600.4 %all-to-all-start = ((bf16[4,6400,512]{2,0,1:T(4,128)(2,1)}), bf16[4,6400,512]{2,0,1:T(4,128)(2,1)}, u32[]{:S(2)}, u32[]{:S(2)}) async-start(bf16[4,6400,512]{2,0,1:T(4,128)(2,1)} %copy.18), calls=%async_computation | async-start | bytes 52428800 | tf_op jit(solution)/shard_map/all_to_all | solution.py:12
Sparse Core Ops, SparseCore 0:
  33.9 135.4 all-reduce.1
where the time goes:
time: 907 us; the launch traced here: 906 us
  blocking collectives  590 us (65%)
  waiting for transfers between devices  136 us (15%)
  local copies, waits for them, and re-layouts  100 us (11%)
  other arithmetic  58.5 us (6%)
  between operations  14.1 us (2%)
    all_gather x1, blocking collectives, per_device(): row_router = lax.all_gather(part_router, 'shard', axis=0, tiled=True)  585 us
    psum x1, waiting for transfers between devices, per_device(): total_down = lax.psum(jnp.sum(latest_down * latest_down, axis=2), 'shard')  136 us
    all_to_all x2, local copies, waits for them, and re-layouts, per_device(): lax.all_to_all(narrow_down, 'shard', split_axis=1, concat_axis=2, tiled=T...  57.4 us
    convert_element_type x1, other arithmetic, per_device(): (latest_down / jnp.expand_dims(scale_down, 2)).astype(jnp.bfloat16)  34.3 us
    convert_element_type x1, local copies, waits for them, and re-layouts, per_device(): (latest_down / jnp.expand_dims(scale_down, 2)).astype(jnp.bfloat16)  33.4 us
    reduce_sum x1, other arithmetic, per_device(): total_down = lax.psum(jnp.sum(latest_down * latest_down, axis=2), 'shard')  24.2 us
  transfers between devices with their start and end apart: 2, of which 1 were waited for; matrix products, arithmetic and copies ran while one was open for 0% of the time, Pallas kernels for 0%

commit v1 on v0

--- a/solution.py
+++ b/solution.py
@@ -1,7 +1,15 @@
+import functools
 import jax
 import jax.numpy as jnp
 from jax import lax
 from jax.sharding import PartitionSpec as P
+
+
+def return_all_slabs(x_local, dim_i):
+    return jnp.concatenate(lax.all_gather(x_local, axis_name="expert"), axis=dim_i)
+
+
+stacks_all_set = functools.partial(return_all_slabs, dim_i=1)
 
 
 def per_device(train_down, other_down, router_weight, router_gain):
@@ -15,7 +23,7 @@
     )
     part_router = (router_weight * router_gain[:, None]).astype(jnp.bfloat16)
     row_router = lax.all_gather(part_router, "shard", axis=0, tiled=True)
-    serve_router = lax.all_gather(row_router, "expert", axis=1, tiled=True)
+    serve_router = stacks_all_set(row_router)
     return (ready_down, scale_down, serve_router)
 
 

time: 907 us -> 907 us (level)
  no operation moved by 1% of the time
where the time goes in v1:
time: 907 us; the launch traced here: 906 us
  blocking collectives  590 us (65%)
  waiting for transfers between devices  136 us (15%)
  local copies, waits for them, and re-layouts  100 us (11%)
  other arithmetic  58.5 us (6%)
  between operations  14.1 us (2%)
    all_gather x1, blocking collectives, per_device(): row_router = lax.all_gather(part_router, 'shard', axis=0, tiled=True)  585 us
    psum x1, waiting for transfers between devices, per_device(): total_down = lax.psum(jnp.sum(latest_down * latest_down, axis=2), 'shard')  136 us
    all_to_all x2, local copies, waits for them, and re-layouts, per_device(): lax.all_to_all(narrow_down, 'shard', split_axis=1, concat_axis=2, tiled=T...  57.4 us
    convert_element_type x1, other arithmetic, per_device(): (latest_down / jnp.expand_dims(scale_down, 2)).astype(jnp.bfloat16)  34.3 us
    convert_element_type x1, local copies, waits for them, and re-layouts, per_device(): (latest_down / jnp.expand_dims(scale_down, 2)).astype(jnp.bfloat16)  33.4 us
    reduce_sum x1, other arithmetic, per_device(): total_down = lax.psum(jnp.sum(latest_down * latest_down, axis=2), 'shard')  24.2 us
  transfers between devices with their start and end apart: 2, of which 1 were waited for; matrix products, arithmetic and copies ran while one was open for 0% of the time, Pallas kernels for 0%

profile of v1, /device:TPU:0, one launch (start us, length us, event | category | flops | bytes accessed | tf_op | source)
XLA Modules:
  0.0 905.5 jit_solution(448214093036344014)
XLA Ops:
  7.2 0.0 all-reduce.2.cloned.1.call-start
  7.2 24.2 %multiply_reduce_fusion = f32[4,6400]{1,0:T(4,128)S(1)} fusion(f32[4,6400,512]{2,1,0:T(8,128)} %param.4, bf16[4,6400,512]{2,1,0:T(8,128)(2,1)} %param.5), kind=kLoop, calls=%fused_computation.1 | loop fusion | flops 52403200 | bytes 78745600 | tf_op jit(solution)/shard_map/reduce_sum | solution.py:17
  31.4 2.3 copy.25
  33.7 0.0 all-reduce.2.cloned.1.call-update
  33.7 135.6 %all-reduce.2.cloned.1.call-done = f32[4,6400]{0,1:T(8,128)} async-done(((f32[4,6400]{0,1:T(8,128)}), f32[4,6400]{0,1:T(8,128)}) %all-reduce.2.cloned.1.call-update) | async-done | bytes 102416 | tf_op jit(solution)/shard_map/psum | solution.py:17
  169.3 2.7 sqrt.3
  172.0 1.2 copy.20
  173.3 34.3 %divide_convert_fusion = bf16[4,6400,512]{2,1,0:T(8,128)(2,1)} fusion(f32[4,6400,512]{2,1,0:T(8,128)} %param.4, bf16[4,6400,512]{2,1,0:T(8,128)(2,1)} %param.5, f32[4,6400]{1,0:T(4,128)S(1)} %copy.20), kind=kLoop, calls=%fused_computation | loop fusion | flops 52428800 | bytes 104960000 | tf_op jit(solution)/shard_map/convert_element_type | solution.py:19
  207.5 33.4 %copy.21 = bf16[4,6400,512]{2,0,1:T(4,128)(2,1)} copy(bf16[4,6400,512]{2,1,0:T(8,128)(2,1)} %divide_convert_fusion) | data formatting | bytes 52428800 | tf_op jit(solution)/shard_map/convert_element_type | solution.py:19
  240.9 0.0 copy-start
  240.9 0.0 copy-start.1
  240.9 6.6 all-to-all-start
  247.6 0.0 copy-done
  247.6 0.0 copy-done.1
  247.6 585.0 %all_gather.9 = bf16[4096,4]{0,1:T(4,128)(2,1)S(1)} all-gather(bf16[512,4]{0,1:T(4,128)(2,1)S(1)} %multiply_convert_fusion), channel_id=1, replica_groups=mesh['expert'=4,'shard'=8] {'shard'}, dimensions={0}, use_global_device_ids=true | all-gather | bytes 36864 | tf_op jit(solution)/shard_map/all_gather | solution.py:25
  832.7 5.4 all-gather
  838.1 0.7 reshape.15
  838.8 0.8 constant_dynamic-slice_fusion
  839.5 1.8 copy.24
  841.3 0.0 all-to-all-done
  841.3 18.2 %copy.22 = bf16[4,800,8,512]{3,2,1,0:T(8,128)(2,1)} copy(bf16[4,800,8,512]{3,0,1,2:T(4,128)(2,1)} %bitcast.1) | data formatting | bytes 52428800 | tf_op jit(solution)/shard_map/all_to_all | solution.py:20
  859.5 39.2 %all_to_all.16 = bf16[4,800,4096]{2,1,0:T(8,128)(2,1)} reshape(bf16[4,800,8,512]{3,2,1,0:T(8,128)(2,1)} %copy.22) | data formatting | bytes 52428800 | tf_op jit(solution)/shard_map/all_to_all | solution.py:20
  (1 shorter events, 0.0 us)
Async XLA Ops:
  7.2 162.2 %all-reduce.2.cloned.1.call-start = ((), (), s32[]{:S(2)}) async-start(), calls=%async_computation.1 | async-start | bytes 6553600 | tf_op jit(solution)/shard_map/psum | solution.py:17
  240.9 6.7 copy-start
  240.9 6.7 copy-start.1
  240.9 600.4 %all-to-all-start = ((bf16[4,6400,512]{2,0,1:T(4,128)(2,1)}), bf16[4,6400,512]{2,0,1:T(4,128)(2,1)}, u32[]{:S(2)}, u32[]{:S(2)}) async-start(bf16[4,6400,512]{2,0,1:T(4,128)(2,1)} %copy.21), calls=%async_computation | async-start | bytes 52428800 | tf_op jit(solution)/shard_map/all_to_all | solution.py:20
Sparse Core Ops, SparseCore 0:
  33.9 135.4 all-reduce.1

commit v2 on v0

--- a/solution.py
+++ b/solution.py
@@ -1,12 +1,21 @@
+import functools
 import jax
 import jax.numpy as jnp
 from jax import lax
 from jax.sharding import PartitionSpec as P
+from jax.lax import all_gather
+
+
+def ends_answer(sheet, axis_id):
+    return jnp.sum(all_gather(sheet, axis_id), axis=0)
+
+
+get_stocks = functools.partial(ends_answer, axis_id="shard")
 
 
 def per_device(train_down, other_down, router_weight, router_gain):
     latest_down = train_down + other_down.astype(jnp.float32)
-    total_down = lax.psum(jnp.sum(latest_down * latest_down, axis=2), "shard")
+    total_down = get_stocks(jnp.sum(latest_down * latest_down, axis=2))
     scale_down = jnp.sqrt(total_down)
     narrow_down = (latest_down / jnp.expand_dims(scale_down, 2)).astype(jnp.bfloat16)
     ready_down = lax.all_to_all(narrow_down, "shard", split_axis=1, concat_axis=2, tiled=True)

time: 907 us -> 781 us (0.86)
  waiting for transfers between devices: 136 us -> 0.01 us
  blocking collectives: 590 us -> 620 us
  between operations: 14.1 us -> 0.71 us
    psum x1 -> x0, waiting for transfers between devices: 136 us -> none  [per_device(): total_down = lax.psum(jnp.sum(latest_down * latest_down, axis=2), 'shard')]
    all_gather x0 -> x1, blocking collectives: none -> 33.9 us  [ends_answer(): return jnp.sum(all_gather(sheet, axis_id), axis=0)]
    reduce_sum x1 -> x2, other arithmetic: 24.2 us -> 24.4 us  [the longest x1 24.2 us: per_device(): total_down = get_stocks(jnp.sum(latest_down * latest_down, axis=2))]
  transfers between devices with their start and end apart: 2 -> 1, of which waited for: 1 -> 0; matrix products, arithmetic and copies ran while one was open for 0% -> 0% of each run, Pallas kernels for 0% -> 0%
where the time goes in v2:
time: 781 us; the launch traced here: 780 us
  blocking collectives  620 us (79%)
  local copies, waits for them, and re-layouts  94.5 us (12%)
  other arithmetic  58.7 us (8%)
    all_gather x1, blocking collectives, per_device(): row_router = lax.all_gather(part_router, 'shard', axis=0, tiled=True)  580 us
    all_to_all x2, local copies, waits for them, and re-layouts, per_device(): lax.all_to_all(narrow_down, 'shard', split_axis=1, concat_axis=2, tiled=T...  57.4 us
    convert_element_type x1, other arithmetic, per_device(): (latest_down / jnp.expand_dims(scale_down, 2)).astype(jnp.bfloat16)  34.3 us
    all_gather x1, blocking collectives, ends_answer(): return jnp.sum(all_gather(sheet, axis_id), axis=0)  33.9 us
    convert_element_type x1, local copies, waits for them, and re-layouts, per_device(): (latest_down / jnp.expand_dims(scale_down, 2)).astype(jnp.bfloat16)  33.4 us
    reduce_sum x1, other arithmetic, per_device(): total_down = get_stocks(jnp.sum(latest_down * latest_down, axis=2))  24.2 us
  transfers between devices with their start and end apart: 1, of which 0 were waited for; matrix products, arithmetic and copies ran while one was open for 0% of the time, Pallas kernels for 0%

profile of v2, /device:TPU:0, one launch (start us, length us, event | category | flops | bytes accessed | tf_op | source)
XLA Modules:
  0.0 780.0 jit_solution(1847130021066882002)
XLA Ops:
  0.6 24.2 %multiply_reduce_fusion = f32[4,6400]{1,0:T(4,128)S(1)} fusion(f32[4,6400,512]{2,1,0:T(8,128)} %param.4, bf16[4,6400,512]{2,1,0:T(8,128)(2,1)} %param.5), kind=kLoop, calls=%fused_computation.1 | loop fusion | flops 52403200 | bytes 78745600 | tf_op jit(solution)/shard_map/reduce_sum | solution.py:18
  24.9 1.1 copy.21
  26.0 1.2 copy.18
  27.2 33.9 %all-gather.1 = f32[8,4,6400]{2,1,0:T(4,128)S(1)} all-gather(f32[1,4,6400]{2,1,0:T(4,128)S(1)} %copy.18), channel_id=2, replica_groups=mesh['expert'=4,'shard'=8] {'shard'}, dimensions={0}, use_global_device_ids=true | all-gather | bytes 921600 | tf_op jit(solution)/shard_map/all_gather | solution.py:10
  61.2 0.1 reduce_sum.19
  61.3 0.1 sqrt.7
  61.4 34.3 %divide_convert_fusion = bf16[4,6400,512]{2,1,0:T(8,128)(2,1)} fusion(f32[4,6400,512]{2,1,0:T(8,128)} %param.4, bf16[4,6400,512]{2,1,0:T(8,128)(2,1)} %param.5, f32[4,6400]{1,0:T(4,128)S(1)} %sqrt.7), kind=kLoop, calls=%fused_computation | loop fusion | flops 52428800 | bytes 104960000 | tf_op jit(solution)/shard_map/convert_element_type | solution.py:20
  95.6 0.0 copy-start
  95.6 0.0 copy-start.1
  95.7 33.4 %copy.19 = bf16[4,6400,512]{2,0,1:T(4,128)(2,1)} copy(bf16[4,6400,512]{2,1,0:T(8,128)(2,1)} %divide_convert_fusion) | data formatting | bytes 52428800 | tf_op jit(solution)/shard_map/convert_element_type | solution.py:20
  129.0 6.5 all-to-all-start
  135.5 0.0 copy-done
  135.6 0.0 copy-done.1
  135.6 580.2 %all_gather.14 = bf16[4096,4]{0,1:T(4,128)(2,1)S(1)} all-gather(bf16[512,4]{0,1:T(4,128)(2,1)S(1)} %multiply_convert_fusion), channel_id=1, replica_groups=mesh['expert'=4,'shard'=8] {'shard'}, dimensions={0}, use_global_device_ids=true | all-gather | bytes 36864 | tf_op jit(solution)/shard_map/all_gather | solution.py:26
  715.8 5.4 all-gather.2
  721.2 0.7 reshape.14
  721.9 0.7 constant_dynamic-slice_fusion
  722.6 0.0 all-to-all-done
  722.6 18.2 %copy.20 = bf16[4,800,8,512]{3,2,1,0:T(8,128)(2,1)} copy(bf16[4,800,8,512]{3,0,1,2:T(4,128)(2,1)} %bitcast.2) | data formatting | bytes 52428800 | tf_op jit(solution)/shard_map/all_to_all | solution.py:21
  740.8 39.2 %all_to_all.16 = bf16[4,800,4096]{2,1,0:T(8,128)(2,1)} reshape(bf16[4,800,8,512]{3,2,1,0:T(8,128)(2,1)} %copy.20) | data formatting | bytes 52428800 | tf_op jit(solution)/shard_map/all_to_all | solution.py:21
  (1 shorter events, 0.0 us)
Async XLA Ops:
  95.6 39.9 %copy-start = (f32[512,4]{0,1:T(4,128)S(1)}, f32[512,4]{0,1:T(4,128)}, u32[]{:S(2)}) copy-start(f32[512,4]{0,1:T(4,128)} %param.6) | copy-start | bytes 24580
  95.6 39.9 %copy-start.1 = (f32[512]{0:T(512)S(1)}, f32[512]{0:T(512)}, u32[]{:S(2)}) copy-start(f32[512]{0:T(512)} %param.7) | copy-start | bytes 6148
  129.0 593.6 %all-to-all-start = ((bf16[4,6400,512]{2,0,1:T(4,128)(2,1)}), bf16[4,6400,512]{2,0,1:T(4,128)(2,1)}, u32[]{:S(2)}, u32[]{:S(2)}) async-start(bf16[4,6400,512]{2,0,1:T(4,128)(2,1)} %copy.19), calls=%async_computation | async-start | bytes 52428800 | tf_op jit(solution)/shard_map/all_to_all | solution.py:21
